TPU v7x, 128 devices: a whole 4x4x4 slice. The times are simulated.
128 devices in a mesh: col: 16 (over y, z), row: 8 (over x, core).
Axes of the slice: x: 4, y: 4, z: 4, core: 2. Of those that a mesh axis runs over, the one named last changes fastest.
Arguments:
- u_factors: bfloat16 [2, 64, 256, 64, 128], P(None, 'row', None, 'col'), may hold values from -0.09375 to 0.09375
- v_factors: bfloat16 [2, 64, 256, 64, 128], P(None, 'row', None, 'col'), may hold values from -0.375 to 0.375
- ranks: int32 [2, 64, 64], P(None, 'row', 'col'), may hold values from 8 to 64
- model_init: float32 [2, 16384, 256], P(None, ('col', 'row')), may hold values from -6 to 6
- observed: float32 [2, 16384, 256], P(None, ('row', 'col')), may hold values from -6 to 6
- step: float32 [2], replicated, may hold values from 0.1 to 0.4
Outputs:
- model: float32 [2, 16384, 256], P(None, ('col', 'row'))
- misfit: float32 [2, 16384, 256], P(None, ('row', 'col'))
Inputs may be any that keep to these rules, and one draw needn't show every extreme that they name: `ranks`: columns of a factor beyond its tile's rank do not count.
All inputs are finite; a program needn't handle non-finite values.
Results may differ from a plain program's by a relative error of at most 0.0085.
Values may be sent and summed in bfloat16 or wider, within the bound.
A program may use at most 128 MiB of HBM per device.

v0:
```python
import jax
import jax.numpy as jnp
from jax import lax
from jax.sharding import PartitionSpec as P

ITERS = 2


def split_product(product, rank_mask, rank_most, right_count):
    real = product[..., :rank_most, :right_count] + product[..., rank_most:, right_count:]
    imaginary = product[..., :rank_most, right_count:] - product[..., rank_most:, :right_count]
    weights = rank_mask[..., None]
    return jnp.concatenate([real * weights, imaginary * weights], -1).astype(jnp.bfloat16)


def expand_complex(coefficient, right_count):
    real = coefficient[..., :right_count]
    imaginary = coefficient[..., right_count:]
    upper = jnp.concatenate([real, imaginary], -1)
    lower = jnp.concatenate([-imaginary, real], -1)
    return jnp.concatenate([upper, lower], -2)


def local(u_factors, v_factors, ranks, model_init, observed, step):
    frequencies = model_init.shape[0]
    rank_most = u_factors.shape[-1] // 2
    right_count = model_init.shape[-1] // 2
    tile_size = u_factors.shape[2]
    rows_here = u_factors.shape[1]
    cols_here = u_factors.shape[3]
    rank_mask = (
        jnp.arange(rank_most, dtype=jnp.int32)[None, None, None, :] < ranks[..., None]
    ).astype(jnp.float32)
    model = model_init
    misfit = model_init
    observed_block = lax.all_gather(observed, "col", axis=1, tiled=True)
    for sweep in range(ITERS):
        gathered = lax.all_gather(model.astype(jnp.bfloat16), "row", axis=1, tiled=True)
        model_tiles = gathered.reshape(frequencies, cols_here, tile_size, 2 * right_count)
        product = jnp.einsum(
            "fiajk,fjal->fijkl", v_factors, model_tiles, preferred_element_type=jnp.float32
        )
        coefficient = expand_complex(
            split_product(product, rank_mask, rank_most, right_count), right_count
        )
        partial_value = jnp.einsum(
            "fiajk,fijkl->fial", u_factors, coefficient, preferred_element_type=jnp.float32
        )
        partial_value = partial_value.reshape(frequencies, rows_here * tile_size, 2 * right_count)
        predicted = lax.psum(partial_value, "col")
        full_misfit = predicted - observed_block
        misfit_half = full_misfit.astype(jnp.bfloat16)
        share = observed.shape[1]
        misfit = lax.dynamic_slice_in_dim(full_misfit, lax.axis_index("col") * share, share, 1)
        misfit_tiles = misfit_half.reshape(frequencies, rows_here, tile_size, 2 * right_count)
        product = jnp.einsum(
            "fiajk,fial->fijkl", u_factors, misfit_tiles, preferred_element_type=jnp.float32
        )
        back = expand_complex(
            split_product(product, rank_mask, rank_most, right_count), right_count
        )
        gradient_part = jnp.einsum(
            "fiajk,fijkl->fjal", v_factors, back, preferred_element_type=jnp.float32
        )
        gradient_part = gradient_part.reshape(frequencies, cols_here * tile_size, 2 * right_count)
        gradient = lax.psum_scatter(gradient_part, "row", scatter_dimension=1, tiled=True)
        model = model - step[:, None, None] * gradient
    return (model, misfit)


def solution(mesh):
    return jax.shard_map(
        local,
        mesh=mesh,
        in_specs=(
            P(None, "row", None, "col", None),
            P(None, "row", None, "col", None),
            P(None, "row", "col"),
            P(None, ("col", "row"), None),
            P(None, ("row", "col"), None),
            P(),
        ),
        out_specs=(P(None, ("col", "row"), None), P(None, ("row", "col"), None)),
        check_vma=False,
    )
```

profile of v0, /device:TPU:0, one launch (start us, length us, event | category | flops | bytes accessed | tf_op | source)
XLA Modules:
  0.0 443.3 jit_solution(17294954381206863518)
XLA Ops:
  7.2 1.6 convert_element_type.23
  8.9 7.5 %copy.8 = bf16[2,8,256,4,128]{2,4,1,3,0:T(8,128)(2,1)} copy(bf16[2,8,256,4,128]{4,3,2,1,0:T(4,128)(2,1)} %param.7) | data formatting | bytes 8388608 | tf_op args[1]
  16.4 7.4 %copy.11 = bf16[2,8,256,4,128]{2,4,3,1,0:T(8,128)(2,1)} copy(bf16[2,8,256,4,128]{4,3,2,1,0:T(4,128)(2,1)} %param.6) | data formatting | bytes 8388608 | tf_op args[0]
  23.8 12.1 %all-gather.4.cloned.1.call-done = bf16[2,1024,256]{2,1,0:T(8,128)(2,1)} async-done(((bf16[2,128,256]{2,1,0:T(8,128)(2,1)}), bf16[2,1024,256]{2,1,0:T(8,128)(2,1)}) %all-gather.4.cloned.1.call-update) | async-done | bytes 1048592 | tf_op jit(solution)/shard_map/all_gather | solution.py:38
  36.0 3.7 fusion.49
  41.2 1.5 copy-done
  42.7 2.9 fusion.18
  46.4 103.1 %all-reduce.3.cloned.1.call-done = f32[2,2048,256]{2,1,0:T(8,128)} async-done(((f32[2,2048,256]{2,1,0:T(8,128)}), f32[2,2048,256]{2,1,0:T(8,128)}) %all-reduce.3.cloned.1.call-update) | async-done | bytes 4194320 | tf_op jit(solution)/shard_map/psum | solution.py:50
  149.5 53.4 %all-gather.6.cloned.1.call-done = f32[2,2048,256]{2,1,0:T(8,128)} async-done(((f32[2,128,256]{2,1,0:T(8,128)}), f32[2,2048,256]{2,1,0:T(8,128)}) %all-gather.6.cloned.1.call-update) | async-done | bytes 4194320 | tf_op jit(solution)/shard_map/all_gather | solution.py:36
  202.9 4.3 subtract_convert_fusion
  211.3 1.5 copy-done.4
  212.8 2.8 fusion
  215.6 33.5 %reduce-scatter.3.cloned.1.call-done = f32[2,128,256]{2,1,0:T(8,128)} async-done(((f32[2,1024,256]{2,1,0:T(8,128)}), f32[2,128,256]{2,1,0:T(8,128)}) %reduce-scatter.3.cloned.1.call-update) | async-done | bytes 262160 | tf_op jit(solution)/shard_map/reduce_scatter | solution.py:66
  249.1 1.7 fusion.36
  250.9 22.4 %all-gather.8.cloned.1.call-done = bf16[2,1024,256]{2,1,0:T(8,128)(2,1)} async-done(((bf16[2,128,256]{2,1,0:T(8,128)(2,1)}), bf16[2,1024,256]{2,1,0:T(8,128)(2,1)}) %all-gather.8.cloned.1.call-update) | async-done | bytes 1048592 | tf_op jit(solution)/shard_map/all_gather | solution.py:38
  273.3 3.7 fusion.51
  278.6 1.5 copy-done.2
  280.0 2.9 fusion.16
  283.2 103.7 %all-reduce.5.cloned.1.call-done = f32[2,2048,256]{2,1,0:T(8,128)} async-done(((f32[2,2048,256]{2,1,0:T(8,128)}), f32[2,2048,256]{2,1,0:T(8,128)}) %all-reduce.5.cloned.1.call-update) | async-done | bytes 4194320 | tf_op jit(solution)/shard_map/psum | solution.py:50
  386.8 6.2 %fusion.42 = (bf16[2,2048,256]{2,1,0:T(8,128)(2,1)S(1)}, f32[2,2048,256]{2,1,0:T(8,128)}) fusion(f32[2,2048,256]{2,1,0:T(8,128)} %all-reduce.5.cloned.1.call-done, f32[2,2048,256]{2,1,0:T(8,128)} %all-gather.6.cloned.1.call-done), kind=kLoop, calls=%fused_computation.58 | loop fusion | flops 2097152 | bytes 14680064 | tf_op jit(solution)/shard_map/convert_element_type | solution.py:52
  398.3 2.8 fusion.8
  401.1 1.7 constant_dynamic-slice_fusion
  402.7 32.0 %reduce-scatter.5.cloned.1.call-done = f32[2,128,256]{2,1,0:T(8,128)} async-done(((f32[2,1024,256]{2,1,0:T(8,128)}), f32[2,128,256]{2,1,0:T(8,128)}) %reduce-scatter.5.cloned.1.call-update) | async-done | bytes 262160 | tf_op jit(solution)/shard_map/reduce_scatter | solution.py:66
  434.7 1.8 multiply_subtract_fusion
  (44 shorter events, 13.6 us)
Async XLA Ops:
  7.2 28.8 %all-gather.4.cloned.1.call-start = ((), (), s32[]{:S(2)}) async-start(), calls=%async_computation.2 | async-start | bytes 1179648 | tf_op jit(solution)/shard_map/all_gather | solution.py:38
  8.9 140.7 %all-reduce.3.cloned.1.call-start = ((), (), s32[]{:S(2)}) async-start(), calls=%async_computation.3 | async-start | bytes 8388608 | tf_op jit(solution)/shard_map/psum | solution.py:50
  16.4 7.4 %copy-start.8 = (s32[2,8,4]{1,2,0:T(4,128)S(1)}, s32[2,8,4]{1,2,0:T(4,128)}, u32[]{:S(2)}) copy-start(s32[2,8,4]{1,2,0:T(4,128)} %param.8) | copy-start | bytes 772
  40.5 2.2 copy-start
  45.6 157.3 %all-gather.6.cloned.1.call-start = ((), (), s32[]{:S(2)}) async-start(), calls=%async_computation.4 | async-start | bytes 4456448 | tf_op jit(solution)/shard_map/all_gather | solution.py:36
  46.4 202.7 %reduce-scatter.3.cloned.1.call-start = ((), (), s32[]{:S(2)}) async-start(), calls=%async_computation.5 | async-start | bytes 2359296 | tf_op jit(solution)/shard_map/reduce_scatter | solution.py:66
  202.9 4.6 %copy-start.1 = (bf16[2,8,256,4,128]{2,4,3,1,0:T(8,128)(2,1)S(1)}, bf16[2,8,256,4,128]{2,4,3,1,0:T(8,128)(2,1)}, u32[]{:S(2)}) copy-start(bf16[2,8,256,4,128]{2,4,3,1,0:T(8,128)(2,1)} %copy.11) | copy-start | bytes 12582916
  210.6 2.2 copy-start.4
  212.8 36.3 %copy-start.6 = (f32[2,128,256]{2,1,0:T(8,128)S(1)}, f32[2,128,256]{2,1,0:T(8,128)}, u32[]{:S(2)}) copy-start(f32[2,128,256]{2,1,0:T(8,128)} %param.9) | copy-start | bytes 786436
  212.8 36.3 %copy-start.9 = (f32[2]{0:T(128)S(1)}, f32[2]{0:T(128)}, u32[]{:S(2)}) copy-start(f32[2]{0:T(128)} %param.11) | copy-start | bytes 28
  215.6 57.7 %all-gather.8.cloned.1.call-start = ((), (), s32[]{:S(2)}) async-start(), calls=%async_computation.6 | async-start | bytes 1179648 | tf_op jit(solution)/shard_map/all_gather | solution.py:38
  250.8 136.0 %all-reduce.5.cloned.1.call-start = ((), (), s32[]{:S(2)}) async-start(), calls=%async_computation.7 | async-start | bytes 8388608 | tf_op jit(solution)/shard_map/psum | solution.py:50
  277.8 2.2 copy-start.2
  283.0 151.8 %reduce-scatter.5.cloned.1.call-start = ((), (), s32[]{:S(2)}) async-start(), calls=%async_computation.8 | async-start | bytes 2359296 | tf_op jit(solution)/shard_map/reduce_scatter | solution.py:66
  386.8 6.2 %copy-start.3 = (bf16[2,8,256,4,128]{2,4,3,1,0:T(8,128)(2,1)S(1)}, bf16[2,8,256,4,128]{2,4,3,1,0:T(8,128)(2,1)}, u32[]{:S(2)}) copy-start(bf16[2,8,256,4,128]{2,4,3,1,0:T(8,128)(2,1)} %copy.11) | copy-start | bytes 12582916
  396.1 2.2 copy-start.5
  398.3 36.5 %copy-start.7 = (f32[2,128,256]{2,1,0:T(8,128)S(1)}, f32[2,128,256]{2,1,0:T(8,128)}, u32[]{:S(2)}) copy-start(f32[2,128,256]{2,1,0:T(8,128)} %reduce-scatter.3.cloned.1.call-done) | copy-start | bytes 786436
Sparse Core Ops, SparseCore 0:
  10.2 25.6 all-gather.3
  45.7 103.7 all-reduce.2
  151.7 51.1 all-gather.5
  215.7 33.3 reduce-scatter.2
  251.2 22.0 all-gather.7
  283.1 103.7 all-reduce.4
  401.2 33.4 reduce-scatter.4
where the time goes:
time: 444 us; the launch traced here: 443 us
  waiting for transfers between devices  361 us (81%)
  local copies, waits for them, and re-layouts  24.7 us (6%)
  other arithmetic  21.6 us (5%)
  matrix products  21.4 us (5%)
  between operations  14.3 us (3%)
    psum x2, waiting for transfers between devices, local(): predicted = lax.psum(partial_value, 'col')  207 us
    reduce_scatter x2, waiting for transfers between devices, local(): lax.psum_scatter(gradient_part, 'row', scatter_dimension=1, tiled=True)  65.5 us
    all_gather x1, waiting for transfers between devices, local(): observed_block = lax.all_gather(observed, 'col', axis=1, tiled=True)  53.4 us
    all_gather x2, waiting for transfers between devices, local(): lax.all_gather(model.astype(jnp.bfloat16), 'row', axis=1, tiled=True)  34.6 us
    unnamed x22, local copies, waits for them, and re-layouts  21 us
    convert_element_type x2, other arithmetic, local(): misfit_half = full_misfit.astype(jnp.bfloat16)  10.5 us
    unnamed x4, matrix products  9.98 us
  transfers between devices with their start and end apart: 7, of which 7 were waited for; matrix products, arithmetic and copies ran while one was open for 4% of the time, Pallas kernels for 0%

commit v1 on v0

--- a/solution.py
+++ b/solution.py
@@ -47,7 +47,8 @@
             "fiajk,fijkl->fial", u_factors, coefficient, preferred_element_type=jnp.float32
         )
         partial_value = partial_value.reshape(frequencies, rows_here * tile_size, 2 * right_count)
-        predicted = lax.psum(partial_value, "col")
+        parts = lax.all_gather(partial_value, "col", axis=0, tiled=False)
+        predicted = parts.sum(axis=0)
         full_misfit = predicted - observed_block
         misfit_half = full_misfit.astype(jnp.bfloat16)
         share = observed.shape[1]

time: 444 us -> 996 us (2.24)
  waiting for transfers between devices: 361 us -> 867 us
  other arithmetic: 21.6 us -> 67.9 us
    all_gather x0 -> x2, waiting for transfers between devices: none -> 736 us  [local(): parts = lax.all_gather(partial_value, 'col', axis=0, tiled=False)]
    psum x2 -> x0, waiting for transfers between devices: 207 us -> none  [local(): predicted = lax.psum(partial_value, 'col')]
    reduce_sum x0 -> x2, other arithmetic: none -> 46.3 us  [local(): predicted = parts.sum(axis=0)]
    all_gather x1, waiting for transfers between devices: 53.4 us -> 30 us  [local(): observed_block = lax.all_gather(observed, 'col', axis=1, tiled=True)]
where the time goes in v1:
time: 996 us
  waiting for transfers between devices  867 us (87%)
  other arithmetic  67.9 us (7%)
  local copies, waits for them, and re-layouts  24.7 us (2%)
  matrix products  21.4 us (2%)
  between operations  14.3 us (1%)
    all_gather x2, waiting for transfers between devices, local(): parts = lax.all_gather(partial_value, 'col', axis=0, tiled=False)  736 us
    reduce_scatter x2, waiting for transfers between devices, local(): lax.psum_scatter(gradient_part, 'row', scatter_dimension=1, tiled=True)  65.4 us
    reduce_sum x2, other arithmetic, local(): predicted = parts.sum(axis=0)  46.3 us
    all_gather x2, waiting for transfers between devices, local(): lax.all_gather(model.astype(jnp.bfloat16), 'row', axis=1, tiled=True)  34.6 us
    all_gather x1, waiting for transfers between devices, local(): observed_block = lax.all_gather(observed, 'col', axis=1, tiled=True)  30 us
    unnamed x22, local copies, waits for them, and re-layouts  21 us
  transfers between devices with their start and end apart: 7, of which 7 were waited for; matrix products, arithmetic and copies ran while one was open for 4% of the time, Pallas kernels for 0%

profile of v1, /device:TPU:0, one launch (start us, length us, event | category | flops | bytes accessed | tf_op | source)
XLA Modules:
  0.0 995.8 jit_solution(6100342334582928994)
XLA Ops:
  7.2 1.6 convert_element_type.23
  8.9 7.5 copy.20
  16.4 7.4 copy.23
  23.8 12.2 %all-gather.6.cloned.1.call-done = bf16[2,1024,256]{2,1,0:T(8,128)(2,1)} async-done(((bf16[2,128,256]{2,1,0:T(8,128)(2,1)}), bf16[2,1024,256]{2,1,0:T(8,128)(2,1)}) %all-gather.6.cloned.1.call-update) | async-done | bytes 1048592 | tf_op jit(solution)/shard_map/all_gather | solution.py:38
  36.0 3.7 fusion.49
  41.2 1.5 copy-done
  42.7 2.9 fusion.18
  46.4 367.9 %all-gather.8.cloned.1.call-done = f32[16,2,2048,256]{3,2,1,0:T(8,128)} async-done(((f32[1,2,2048,256]{3,2,1,0:T(8,128)}), f32[16,2,2048,256]{3,2,1,0:T(8,128)}) %all-gather.8.cloned.1.call-update) | async-done | bytes 67108880 | tf_op jit(solution)/shard_map/all_gather | solution.py:50
  414.3 23.3 %reduce_sum.18 = f32[2,2048,256]{2,1,0:T(8,128)} reduce(f32[16,2,2048,256]{3,2,1,0:T(8,128)} %all-gather.8.cloned.1.call-done, f32[]{:T(128)} %constant.2.clone.1), dimensions={0}, to_apply=%region_0.0 | reduce | flops 15728640 | bytes 71303168 | tf_op jit(solution)/shard_map/reduce_sum | solution.py:51
  437.7 30.0 %all-gather.10.cloned.1.call-done = f32[2,2048,256]{2,1,0:T(8,128)} async-done(((f32[2,128,256]{2,1,0:T(8,128)}), f32[2,2048,256]{2,1,0:T(8,128)}) %all-gather.10.cloned.1.call-update) | async-done | bytes 4194320 | tf_op jit(solution)/shard_map/all_gather | solution.py:36
  467.7 4.3 subtract_convert_fusion
  477.5 2.8 fusion
  480.4 33.5 %reduce-scatter.3.cloned.1.call-done = f32[2,128,256]{2,1,0:T(8,128)} async-done(((f32[2,1024,256]{2,1,0:T(8,128)}), f32[2,128,256]{2,1,0:T(8,128)}) %reduce-scatter.3.cloned.1.call-update) | async-done | bytes 262160 | tf_op jit(solution)/shard_map/reduce_scatter | solution.py:67
  513.9 1.7 fusion.36
  515.6 22.4 %all-gather.12.cloned.1.call-done = bf16[2,1024,256]{2,1,0:T(8,128)(2,1)} async-done(((bf16[2,128,256]{2,1,0:T(8,128)(2,1)}), bf16[2,1024,256]{2,1,0:T(8,128)(2,1)}) %all-gather.12.cloned.1.call-update) | async-done | bytes 1048592 | tf_op jit(solution)/shard_map/all_gather | solution.py:38
  538.1 3.7 fusion.51
  544.8 2.9 fusion.16
  547.9 368.5 %all-gather.14.cloned.1.call-done = f32[16,2,2048,256]{3,2,1,0:T(8,128)} async-done(((f32[1,2,2048,256]{3,2,1,0:T(8,128)}), f32[16,2,2048,256]{3,2,1,0:T(8,128)}) %all-gather.14.cloned.1.call-update) | async-done | bytes 67108880 | tf_op jit(solution)/shard_map/all_gather | solution.py:50
  916.4 22.9 %reduce_sum.19 = f32[2,2048,256]{2,1,0:T(8,128)} reduce(f32[16,2,2048,256]{3,2,1,0:T(8,128)} %all-gather.14.cloned.1.call-done, f32[]{:T(128)} %constant.2.clone.1), dimensions={0}, to_apply=%region_2.0 | reduce | flops 15728640 | bytes 71303168 | tf_op jit(solution)/shard_map/reduce_sum | solution.py:51
  939.4 6.2 fusion.42
  950.8 2.8 fusion.8
  953.6 1.7 constant_dynamic-slice_fusion
  955.3 31.9 %reduce-scatter.5.cloned.1.call-done = f32[2,128,256]{2,1,0:T(8,128)} async-done(((f32[2,1024,256]{2,1,0:T(8,128)}), f32[2,128,256]{2,1,0:T(8,128)}) %reduce-scatter.5.cloned.1.call-update) | async-done | bytes 262160 | tf_op jit(solution)/shard_map/reduce_scatter | solution.py:67
  987.2 1.8 multiply_subtract_fusion
  (46 shorter events, 16.5 us)
Async XLA Ops:
  7.2 28.8 %all-gather.6.cloned.1.call-start = ((), (), s32[]{:S(2)}) async-start(), calls=%async_computation.2 | async-start | bytes 1179648 | tf_op jit(solution)/shard_map/all_gather | solution.py:38
  8.9 405.5 %all-gather.8.cloned.1.call-start = ((), (), s32[]{:S(2)}) async-start(), calls=%async_computation.3 | async-start | bytes 71303168 | tf_op jit(solution)/shard_map/all_gather | solution.py:50
  16.4 7.4 copy-start.8
  40.5 2.2 copy-start
  45.6 422.0 %all-gather.10.cloned.1.call-start = ((), (), s32[]{:S(2)}) async-start(), calls=%async_computation.4 | async-start | bytes 4456448 | tf_op jit(solution)/shard_map/all_gather | solution.py:36
  46.4 467.5 %reduce-scatter.3.cloned.1.call-start = ((), (), s32[]{:S(2)}) async-start(), calls=%async_computation.5 | async-start | bytes 2359296 | tf_op jit(solution)/shard_map/reduce_scatter | solution.py:67
  467.7 4.6 copy-start.1
  475.3 2.2 copy-start.4
  477.5 36.3 %copy-start.6 = (f32[2,128,256]{2,1,0:T(8,128)S(1)}, f32[2,128,256]{2,1,0:T(8,128)}, u32[]{:S(2)}) copy-start(f32[2,128,256]{2,1,0:T(8,128)} %param.9) | copy-start | bytes 786436
  477.5 36.3 %copy-start.9 = (f32[2]{0:T(128)S(1)}, f32[2]{0:T(128)}, u32[]{:S(2)}) copy-start(f32[2]{0:T(128)} %param.11) | copy-start | bytes 28
  480.3 57.7 %all-gather.12.cloned.1.call-start = ((), (), s32[]{:S(2)}) async-start(), calls=%async_computation.6 | async-start | bytes 1179648 | tf_op jit(solution)/shard_map/all_gather | solution.py:38
  515.6 400.8 %all-gather.14.cloned.1.call-start = ((), (), s32[]{:S(2)}) async-start(), calls=%async_computation.7 | async-start | bytes 71303168 | tf_op jit(solution)/shard_map/all_gather | solution.py:50
  542.6 2.2 copy-start.2
  547.7 439.5 %reduce-scatter.5.cloned.1.call-start = ((), (), s32[]{:S(2)}) async-start(), calls=%async_computation.8 | async-start | bytes 2359296 | tf_op jit(solution)/shard_map/reduce_scatter | solution.py:67
  939.4 6.2 copy-start.3
  948.6 2.2 copy-start.5
  950.8 36.4 %copy-start.7 = (f32[2,128,256]{2,1,0:T(8,128)S(1)}, f32[2,128,256]{2,1,0:T(8,128)}, u32[]{:S(2)}) copy-start(f32[2,128,256]{2,1,0:T(8,128)} %reduce-scatter.3.cloned.1.call-done) | copy-start | bytes 786436
Sparse Core Ops, SparseCore 0:
  10.2 25.6 all-gather.5
  45.8 368.5 all-gather.7
  416.5 51.0 all-gather.9
  480.4 33.3 reduce-scatter.2
  516.0 22.0 all-gather.11
  547.8 368.5 all-gather.13
  953.7 33.4 reduce-scatter.4
